TPU v7x, 32 devices: a whole 2x2x4 slice. The times are simulated.
32 devices in a mesh: ta: 4 (over z), gz: 2 (over x), xy: 4 (over y, core).
Axes of the slice: x: 2, y: 2, z: 4, core: 2. Of those that a mesh axis runs over, the one named last changes fastest.
Arguments:
- links: float32 [4, 2, 4, 4, 9, 4608], P('ta', 'gz', 'xy'), may hold values from -1 to 3
- eigvecs: float32 [4, 2, 4, 4, 48, 128], P('ta', 'gz', 'xy'), may hold values from -1 to 1
- eig_real: float32 [64], replicated, may hold values from 0.8 to 2.5
- eig_imag: float32 [64], replicated, may hold values from -0.5 to 0.5
- rhs: float32 [4, 2, 4, 4, 48, 128], P('ta', 'gz', 'xy'), may hold values from -3000 to 3000
Outputs:
- solution: float32 [4, 2, 4, 4, 48, 128], P('ta', 'gz', 'xy')
- residual: float32 [4, 2, 4, 4, 48, 128], P('ta', 'gz', 'xy')
All inputs are finite; a program needn't handle non-finite values.
Results may differ from a plain program's by a relative error of at most 0.0003.
Values sent between devices are 32-bit elements; how exact they have to be, the bound alone decides.
A program may use at most 64 MiB of HBM per device.

v0:
```python
import jax
import jax.numpy as jnp
from jax import lax
from jax.sharding import PartitionSpec as P

SWEEPS = 4


HIGH = lax.Precision.HIGHEST


def with_halo(x, sides, width):
    for axis, dim in sides:
        peers, length = (lax.axis_size(axis), x.shape[dim])
        up = [(i, (i + 1) % peers) for i in range(peers)]
        down = [(j, i) for i, j in up]
        last = lax.slice_in_dim(x, length - width, length, axis=dim)
        initial = lax.slice_in_dim(x, 0, width, axis=dim)
        before = lax.ppermute(last, axis, up)
        after = lax.ppermute(initial, axis, down)
        x = jnp.concatenate([before, x, after], axis=dim)
    return x


def operate(links, field):
    dof = field.shape[4]
    half = field.shape[-1] // 2
    padded = with_halo(field, (("ta", 0), ("gz", 1), ("xy", 2)), 1)
    centre = padded[1:-1, 1:-1, 1:-1]
    stacked = jnp.stack(
        [
            centre,
            -padded[2:, 1:-1, 1:-1],
            -padded[1:-1, 2:, 1:-1],
            -padded[1:-1, 1:-1, 2:],
            -jnp.roll(centre, -1, 3),
            -padded[:-2, 1:-1, 1:-1],
            -padded[1:-1, :-2, 1:-1],
            -padded[1:-1, 1:-1, :-2],
            -jnp.roll(centre, 1, 3),
        ],
        4,
    )
    real = jnp.einsum("tzxydoi,tzxydic->tzxyoc", links[..., :dof], stacked, precision=HIGH)
    imag = jnp.einsum("tzxydoi,tzxydic->tzxyoc", links[..., dof:], stacked, precision=HIGH)
    return jnp.concatenate(
        [real[..., :half] - imag[..., half:], real[..., half:] + imag[..., :half]], -1
    )


def complex_scale(alpha_re, alpha_im, field):
    half = field.shape[-1] // 2
    f_re = field[..., :half]
    f_im = field[..., half:]
    return jnp.concatenate(
        [alpha_re * f_re - alpha_im * f_im, alpha_re * f_im + alpha_im * f_re], -1
    )


def sweep_step(image, residual):
    half = residual.shape[-1] // 2
    swapped = jnp.concatenate([residual[..., half:], residual[..., :half]], -1)
    first = jnp.sum(image * residual, axis=(0, 1, 2, 3, 4))
    second = jnp.sum(image * swapped, axis=(0, 1, 2, 3, 4))
    power = jnp.sum(image * image, axis=(0, 1, 2, 3, 4))
    num_re, num_im, den = lax.psum(
        (first[:half] + first[half:], second[:half] - second[half:], power[:half] + power[half:]),
        ("ta", "gz", "xy"),
    )
    return (num_re / den, num_im / den)


def local(links, eigvecs, eig_real, eig_imag, rhs):
    nev = eig_real.shape[0]
    half = rhs.shape[-1] // 2
    dof = rhs.shape[4]
    matrices = links.reshape(links.shape[:5] + (dof, 2 * dof))
    rows = eigvecs.reshape(-1, 2 * nev)
    local_cross = jnp.dot(
        rows.T, rhs.reshape(-1, 2 * half), precision=HIGH, preferred_element_type=jnp.float32
    )
    cross = lax.psum(local_cross, ("ta", "gz", "xy"))
    proj_re = cross[:nev, :half] + cross[nev:, half:]
    proj_im = cross[:nev, half:] - cross[nev:, :half]
    denom = (eig_real * eig_real + eig_imag * eig_imag)[:, None]
    coef_re = (proj_re * eig_real[:, None] + proj_im * eig_imag[:, None]) / denom
    coef_im = (proj_im * eig_real[:, None] - proj_re * eig_imag[:, None]) / denom
    block = jnp.concatenate(
        [jnp.concatenate([coef_re, coef_im], 1), jnp.concatenate([-coef_im, coef_re], 1)], 0
    )
    solution = jnp.dot(rows, block, precision=HIGH, preferred_element_type=jnp.float32).reshape(
        rhs.shape
    )
    residual = rhs - operate(matrices, solution)
    image = operate(matrices, residual)
    for sweep in range(SWEEPS):
        alpha_re, alpha_im = sweep_step(image, residual)
        if sweep + 1 < SWEEPS:
            further = operate(matrices, image)
        solution = solution + complex_scale(alpha_re, alpha_im, residual)
        residual = residual - complex_scale(alpha_re, alpha_im, image)
        if sweep + 1 < SWEEPS:
            image = image - complex_scale(alpha_re, alpha_im, further)
    return (solution, residual)


def solution(mesh):
    in_specs = (
        P("ta", "gz", "xy", None, None, None),
        P("ta", "gz", "xy", None, None, None),
        P(),
        P(),
        P("ta", "gz", "xy", None, None, None),
    )
    out_specs = (P("ta", "gz", "xy", None, None, None), P("ta", "gz", "xy", None, None, None))
    return jax.shard_map(local, mesh=mesh, in_specs=in_specs, out_specs=out_specs, check_vma=False)
```

profile of v0, /device:TPU:0, one launch (start us, length us, event | category | flops | bytes accessed | tf_op | source)
XLA Modules:
  0.0 525.7 jit_solution(15367684334829813068)
XLA Ops:
  8.1 2.0 convolution_bitcast_fusion.10
  10.7 125.6 %all-reduce.6.cloned.1.call-done = f32[128,128]{1,0:T(8,128)} async-done(((f32[128,128]{1,0:T(8,128)}), f32[128,128]{1,0:T(8,128)}) %all-reduce.6.cloned.1.call-update) | async-done | bytes 65552 | tf_op jit(solution)/shard_map/psum | solution.py:82
  137.6 2.9 collective-permute-start.1
  141.9 2.5 collective-permute-done.1
  148.7 7.5 %collective-permute-done.3 = f32[3,1,1,4,48,128]{5,4,3,2,1,0:T(8,128)S(1)} collective-permute-done((f32[3,1,1,4,48,128]{5,4,3,2,1,0:T(8,128)S(1)}, f32[3,1,1,4,48,128]{5,4,3,2,1,0:T(8,128)S(1)}, u32[]{:S(2)}, u32[]{:S(2)}) %collective-permute-start.3) | collective-permute-done | bytes 294944 | tf_op jit(solution)/shard_map/ppermute | solution.py:19
  156.2 4.8 collective-permute-done.2
  161.7 18.4 %collective-permute-done.4 = f32[3,3,1,4,48,128]{5,4,3,2,1,0:T(8,128)S(1)} collective-permute-done((f32[3,3,1,4,48,128]{5,4,3,2,1,0:T(8,128)S(1)}, f32[3,3,1,4,48,128]{5,4,3,2,1,0:T(8,128)S(1)}, u32[]{:S(2)}, u32[]{:S(2)}) %collective-permute-start.4) | collective-permute-done | bytes 884768 | tf_op jit(solution)/shard_map/ppermute | solution.py:20
  180.2 2.9 collective-permute-done.5
  188.2 2.4 collective-permute-start.6
  190.6 3.7 collective-permute-done.7
  197.0 7.8 %collective-permute-done.9 = f32[3,1,1,4,48,128]{5,4,3,2,1,0:T(8,128)S(1)} collective-permute-done((f32[3,1,1,4,48,128]{5,4,3,2,1,0:T(8,128)S(1)}, f32[3,1,1,4,48,128]{5,4,3,2,1,0:T(8,128)S(1)}, u32[]{:S(2)}, u32[]{:S(2)}) %collective-permute-start.9) | collective-permute-done | bytes 294944 | tf_op jit(solution)/shard_map/ppermute | solution.py:19
  204.8 4.5 collective-permute-done.8
  210.1 19.4 %collective-permute-done.10 = f32[3,3,1,4,48,128]{5,4,3,2,1,0:T(8,128)S(1)} collective-permute-done((f32[3,3,1,4,48,128]{5,4,3,2,1,0:T(8,128)S(1)}, f32[3,3,1,4,48,128]{5,4,3,2,1,0:T(8,128)S(1)}, u32[]{:S(2)}, u32[]{:S(2)}) %collective-permute-start.10) | collective-permute-done | bytes 884768 | tf_op jit(solution)/shard_map/ppermute | solution.py:20
  235.6 2.6 collective-permute-done.12
  238.2 3.5 collective-permute-done.13
  244.0 44.6 %all-reduce.3 = (f32[64]{0:T(128)S(1)}, f32[64]{0:T(128)S(1)}, f32[64]{0:T(128)S(1)}) all-reduce(f32[64]{0:T(128)S(1)} %get-tuple-element.116, f32[64]{0:T(128)S(1)} %get-tuple-element.117, f32[64]{0:T(128)S(1)} %slice_add_fusion.13), channel_id=1, replica_groups=mesh['ta'=4,'gz'=2,'xy'=4] {'ta','gz','xy'}, use_global_device_ids=true, to_apply=%region_6.7 | all-reduce | flops 192 | bytes 1536 | tf_op jit(solution)/shard_map/psum | solution.py:66
  289.8 16.9 %collective-permute-done.16 = f32[3,3,1,4,48,128]{5,4,3,2,1,0:T(8,128)S(1)} collective-permute-done((f32[3,3,1,4,48,128]{5,4,3,2,1,0:T(8,128)S(1)}, f32[3,3,1,4,48,128]{5,4,3,2,1,0:T(8,128)S(1)}, u32[]{:S(2)}, u32[]{:S(2)}) %collective-permute-start.16) | collective-permute-done | bytes 884768 | tf_op jit(solution)/shard_map/ppermute | solution.py:20
  306.7 4.8 collective-permute-done.17
  316.2 2.6 collective-permute-start.18
  319.0 37.1 %all-reduce.2 = (f32[64]{0:T(128)S(1)}, f32[64]{0:T(128)S(1)}, f32[64]{0:T(128)S(1)}) all-reduce(f32[64]{0:T(128)S(1)} %slice_subtract_fusion.8, f32[64]{0:T(128)S(1)} %slice_add_fusion.10, f32[64]{0:T(128)S(1)} %slice_add_fusion.11), channel_id=1, replica_groups=mesh['ta'=4,'gz'=2,'xy'=4] {'ta','gz','xy'}, use_global_device_ids=true, to_apply=%region_12.13 | all-reduce | flops 192 | bytes 1536 | tf_op jit(solution)/shard_map/psum | solution.py:66
  356.2 2.3 collective-permute-start.21
  358.7 7.6 %collective-permute-done.21 = f32[3,1,1,4,48,128]{5,4,3,2,1,0:T(8,128)S(1)} collective-permute-done((f32[3,1,1,4,48,128]{5,4,3,2,1,0:T(8,128)S(1)}, f32[3,1,1,4,48,128]{5,4,3,2,1,0:T(8,128)S(1)}, u32[]{:S(2)}, u32[]{:S(2)}) %collective-permute-start.21) | collective-permute-done | bytes 294944 | tf_op jit(solution)/shard_map/ppermute | solution.py:19
  366.4 4.1 collective-permute-done.20
  371.2 18.8 %collective-permute-done.22 = f32[3,3,1,4,48,128]{5,4,3,2,1,0:T(8,128)S(1)} collective-permute-done((f32[3,3,1,4,48,128]{5,4,3,2,1,0:T(8,128)S(1)}, f32[3,3,1,4,48,128]{5,4,3,2,1,0:T(8,128)S(1)}, u32[]{:S(2)}, u32[]{:S(2)}) %collective-permute-start.22) | collective-permute-done | bytes 884768 | tf_op jit(solution)/shard_map/ppermute | solution.py:20
  390.1 2.1 collective-permute-done.23
  395.6 2.6 collective-permute-start.25
  399.7 3.3 collective-permute-done.25
  404.0 2.1 collective-permute-start.27
  406.3 46.3 %all-reduce.1 = (f32[64]{0:T(128)S(1)}, f32[64]{0:T(128)S(1)}, f32[64]{0:T(128)S(1)}) all-reduce(f32[64]{0:T(128)S(1)} %slice_subtract_fusion.7, f32[64]{0:T(128)S(1)} %slice_add_fusion.8, f32[64]{0:T(128)S(1)} %slice_add_fusion.9), channel_id=1, replica_groups=mesh['ta'=4,'gz'=2,'xy'=4] {'ta','gz','xy'}, use_global_device_ids=true, to_apply=%region_18.19 | all-reduce | flops 192 | bytes 1536 | tf_op jit(solution)/shard_map/psum | solution.py:66
  453.7 17.2 %collective-permute-done.28 = f32[3,3,1,4,48,128]{5,4,3,2,1,0:T(8,128)S(1)} collective-permute-done((f32[3,3,1,4,48,128]{5,4,3,2,1,0:T(8,128)S(1)}, f32[3,3,1,4,48,128]{5,4,3,2,1,0:T(8,128)S(1)}, u32[]{:S(2)}, u32[]{:S(2)}) %collective-permute-start.28) | collective-permute-done | bytes 884768 | tf_op jit(solution)/shard_map/ppermute | solution.py:20
  470.9 4.7 collective-permute-done.29
  479.3 37.9 %all-reduce = (f32[64]{0:T(128)S(1)}, f32[64]{0:T(128)S(1)}, f32[64]{0:T(128)S(1)}) all-reduce(f32[64]{0:T(128)S(1)} %slice_subtract_fusion.6, f32[64]{0:T(128)S(1)} %slice_add_fusion.6, f32[64]{0:T(128)S(1)} %slice_add_fusion.7), channel_id=1, replica_groups=mesh['ta'=4,'gz'=2,'xy'=4] {'ta','gz','xy'}, use_global_device_ids=true, to_apply=%region_24.25 | all-reduce | flops 192 | bytes 1536 | tf_op jit(solution)/shard_map/psum | solution.py:66
  (156 shorter events, 45.4 us)
Async XLA Ops:
  7.2 134.3 %copy-start.1 = (f32[1,1,1,4,9,4608]{5,3,4,2,1,0:T(4,128)S(1)}, f32[1,1,1,4,9,4608]{5,3,4,2,1,0:T(4,128)}, u32[]{:S(2)}) copy-start(f32[1,1,1,4,9,4608]{5,3,4,2,1,0:T(4,128)} %param.5) | copy-start | bytes 1990660
  7.2 129.1 %all-reduce.6.cloned.1.call-start = ((), (), s32[]{:S(2)}) async-start(), calls=%async_computation | async-start | bytes 131072 | tf_op jit(solution)/shard_map/psum | solution.py:82
  137.6 6.9 %collective-permute-start.1 = (f32[1,1,1,4,48,128]{5,4,3,2,1,0:T(8,128)S(1)}, f32[1,1,1,4,48,128]{5,4,3,2,1,0:T(8,128)S(1)}, u32[]{:S(2)}, u32[]{:S(2)}) collective-permute-start(f32[1,1,1,4,48,128]{5,4,3,2,1,0:T(8,128)S(1)} %bitcast.301), channel_id=1, source_target_pairs={{0,8},{8,16},{16,24},{24,0},{1,9},{9,17},{17,25},{25,1},{2,10},{10... | collective-permute-start | bytes 294920 | tf_op jit(solution)/shard_map/ppermute | solution.py:19
  140.5 5.7 %collective-permute-start = (f32[1,1,1,4,48,128]{5,4,3,2,1,0:T(8,128)S(1)}, f32[1,1,1,4,48,128]{5,4,3,2,1,0:T(8,128)S(1)}, u32[]{:S(2)}, u32[]{:S(2)}) collective-permute-start(f32[1,1,1,4,48,128]{5,4,3,2,1,0:T(8,128)S(1)} %bitcast.302), channel_id=1, source_target_pairs={{8,0},{16,8},{24,16},{0,24},{9,1},{17,9},{25,17},{1,25},{10,2},{18... | collective-permute-start | bytes 294920 | tf_op jit(solution)/shard_map/ppermute | solution.py:20
  146.3 9.9 %collective-permute-start.3 = (f32[3,1,1,4,48,128]{5,4,3,2,1,0:T(8,128)S(1)}, f32[3,1,1,4,48,128]{5,4,3,2,1,0:T(8,128)S(1)}, u32[]{:S(2)}, u32[]{:S(2)}) collective-permute-start(f32[3,1,1,4,48,128]{5,4,3,2,1,0:T(8,128)S(1)} %pad_maximum_fusion.5), channel_id=1, source_target_pairs={{0,4},{4,0},{1,5},{5,1},{2,6},{6,2},{3,7},{7,3},{8,12},{12,8},{9,1... | collective-permute-start | bytes 884744 | tf_op jit(solution)/shard_map/ppermute | solution.py:19
  147.8 13.2 %collective-permute-start.2 = (f32[3,1,1,4,48,128]{5,4,3,2,1,0:T(8,128)S(1)}, f32[3,1,1,4,48,128]{5,4,3,2,1,0:T(8,128)S(1)}, u32[]{:S(2)}, u32[]{:S(2)}) collective-permute-start(f32[3,1,1,4,48,128]{5,4,3,2,1,0:T(8,128)S(1)} %pad_maximum_fusion.5), channel_id=1, source_target_pairs={{4,0},{0,4},{5,1},{1,5},{6,2},{2,6},{7,3},{3,7},{12,8},{8,12},{13,... | collective-permute-start | bytes 884744 | tf_op jit(solution)/shard_map/ppermute | solution.py:20
  161.1 19.1 %collective-permute-start.4 = (f32[3,3,1,4,48,128]{5,4,3,2,1,0:T(8,128)S(1)}, f32[3,3,1,4,48,128]{5,4,3,2,1,0:T(8,128)S(1)}, u32[]{:S(2)}, u32[]{:S(2)}) collective-permute-start(f32[3,3,1,4,48,128]{5,4,3,2,1,0:T(8,128)S(1)} %pad_maximum_fusion), channel_id=1, source_target_pairs={{1,0},{2,1},{3,2},{0,3},{5,4},{6,5},{7,6},{4,7},{9,8},{10,9},{11,1... | collective-permute-start | bytes 2654216 | tf_op jit(solution)/shard_map/ppermute | solution.py:20
  161.2 21.9 %collective-permute-start.5 = (f32[3,3,1,4,48,128]{5,4,3,2,1,0:T(8,128)S(1)}, f32[3,3,1,4,48,128]{5,4,3,2,1,0:T(8,128)S(1)}, u32[]{:S(2)}, u32[]{:S(2)}) collective-permute-start(f32[3,3,1,4,48,128]{5,4,3,2,1,0:T(8,128)S(1)} %pad_maximum_fusion), channel_id=1, source_target_pairs={{0,1},{1,2},{2,3},{3,0},{4,5},{5,6},{6,7},{7,4},{8,9},{9,10},{10,1... | collective-permute-start | bytes 2654216 | tf_op jit(solution)/shard_map/ppermute | solution.py:19
  186.7 7.6 %collective-permute-start.7 = (f32[1,1,1,4,48,128]{5,4,3,2,1,0:T(8,128)S(1)}, f32[1,1,1,4,48,128]{5,4,3,2,1,0:T(8,128)S(1)}, u32[]{:S(2)}, u32[]{:S(2)}) collective-permute-start(f32[1,1,1,4,48,128]{5,4,3,2,1,0:T(8,128)S(1)} %get-tuple-element.34), channel_id=1, source_target_pairs={{0,8},{8,16},{16,24},{24,0},{1,9},{9,17},{17,25},{25,1},{2,10},{10... | collective-permute-start | bytes 294920 | tf_op jit(solution)/shard_map/ppermute | solution.py:19
  188.2 6.6 %collective-permute-start.6 = (f32[1,1,1,4,48,128]{5,4,3,2,1,0:T(8,128)S(1)}, f32[1,1,1,4,48,128]{5,4,3,2,1,0:T(8,128)S(1)}, u32[]{:S(2)}, u32[]{:S(2)}) collective-permute-start(f32[1,1,1,4,48,128]{5,4,3,2,1,0:T(8,128)S(1)} %get-tuple-element.34), channel_id=1, source_target_pairs={{8,0},{16,8},{24,16},{0,24},{9,1},{17,9},{25,17},{1,25},{10,2},{18... | collective-permute-start | bytes 294920 | tf_op jit(solution)/shard_map/ppermute | solution.py:20
  194.9 9.9 %collective-permute-start.9 = (f32[3,1,1,4,48,128]{5,4,3,2,1,0:T(8,128)S(1)}, f32[3,1,1,4,48,128]{5,4,3,2,1,0:T(8,128)S(1)}, u32[]{:S(2)}, u32[]{:S(2)}) collective-permute-start(f32[3,1,1,4,48,128]{5,4,3,2,1,0:T(8,128)S(1)} %pad_maximum_fusion.6), channel_id=1, source_target_pairs={{0,4},{4,0},{1,5},{5,1},{2,6},{6,2},{3,7},{7,3},{8,12},{12,8},{9,1... | collective-permute-start | bytes 884744 | tf_op jit(solution)/shard_map/ppermute | solution.py:19
  196.1 13.2 %collective-permute-start.8 = (f32[3,1,1,4,48,128]{5,4,3,2,1,0:T(8,128)S(1)}, f32[3,1,1,4,48,128]{5,4,3,2,1,0:T(8,128)S(1)}, u32[]{:S(2)}, u32[]{:S(2)}) collective-permute-start(f32[3,1,1,4,48,128]{5,4,3,2,1,0:T(8,128)S(1)} %pad_maximum_fusion.6), channel_id=1, source_target_pairs={{4,0},{0,4},{5,1},{1,5},{6,2},{2,6},{7,3},{3,7},{12,8},{8,12},{13,... | collective-permute-start | bytes 884744 | tf_op jit(solution)/shard_map/ppermute | solution.py:20
  209.3 20.1 %collective-permute-start.10 = (f32[3,3,1,4,48,128]{5,4,3,2,1,0:T(8,128)S(1)}, f32[3,3,1,4,48,128]{5,4,3,2,1,0:T(8,128)S(1)}, u32[]{:S(2)}, u32[]{:S(2)}) collective-permute-start(f32[3,3,1,4,48,128]{5,4,3,2,1,0:T(8,128)S(1)} %pad_maximum_fusion.1), channel_id=1, source_target_pairs={{1,0},{2,1},{3,2},{0,3},{5,4},{6,5},{7,6},{4,7},{9,8},{10,9},{11,1... | collective-permute-start | bytes 2654216 | tf_op jit(solution)/shard_map/ppermute | solution.py:20
  209.5 20.7 %collective-permute-start.11 = (f32[3,3,1,4,48,128]{5,4,3,2,1,0:T(8,128)S(1)}, f32[3,3,1,4,48,128]{5,4,3,2,1,0:T(8,128)S(1)}, u32[]{:S(2)}, u32[]{:S(2)}) collective-permute-start(f32[3,3,1,4,48,128]{5,4,3,2,1,0:T(8,128)S(1)} %pad_maximum_fusion.1), channel_id=1, source_target_pairs={{0,1},{1,2},{2,3},{3,0},{4,5},{5,6},{6,7},{7,4},{8,9},{9,10},{10,1... | collective-permute-start | bytes 2654216 | tf_op jit(solution)/shard_map/ppermute | solution.py:19
  233.4 4.8 collective-permute-start.12
  235.3 6.4 %collective-permute-start.13 = (f32[1,1,1,4,48,128]{5,4,3,2,1,0:T(8,128)S(1)}, f32[1,1,1,4,48,128]{5,4,3,2,1,0:T(8,128)S(1)}, u32[]{:S(2)}, u32[]{:S(2)}) collective-permute-start(f32[1,1,1,4,48,128]{5,4,3,2,1,0:T(8,128)S(1)} %get-tuple-element.32), channel_id=1, source_target_pairs={{0,8},{8,16},{16,24},{24,0},{1,9},{9,17},{17,25},{25,1},{2,10},{10... | collective-permute-start | bytes 294920 | tf_op jit(solution)/shard_map/ppermute | solution.py:19
  241.8 46.8 %collective-permute-start.15 = (f32[3,1,1,4,48,128]{5,4,3,2,1,0:T(8,128)S(1)}, f32[3,1,1,4,48,128]{5,4,3,2,1,0:T(8,128)S(1)}, u32[]{:S(2)}, u32[]{:S(2)}) collective-permute-start(f32[3,1,1,4,48,128]{5,4,3,2,1,0:T(8,128)S(1)} %pad_maximum_fusion.7), channel_id=1, source_target_pairs={{0,4},{4,0},{1,5},{5,1},{2,6},{6,2},{3,7},{7,3},{8,12},{12,8},{9,1... | collective-permute-start | bytes 884744 | tf_op jit(solution)/shard_map/ppermute | solution.py:19
  243.6 45.0 %collective-permute-start.14 = (f32[3,1,1,4,48,128]{5,4,3,2,1,0:T(8,128)S(1)}, f32[3,1,1,4,48,128]{5,4,3,2,1,0:T(8,128)S(1)}, u32[]{:S(2)}, u32[]{:S(2)}) collective-permute-start(f32[3,1,1,4,48,128]{5,4,3,2,1,0:T(8,128)S(1)} %pad_maximum_fusion.7), channel_id=1, source_target_pairs={{4,0},{0,4},{5,1},{1,5},{6,2},{2,6},{7,3},{3,7},{12,8},{8,12},{13,... | collective-permute-start | bytes 884744 | tf_op jit(solution)/shard_map/ppermute | solution.py:20
  288.7 17.9 %collective-permute-start.16 = (f32[3,3,1,4,48,128]{5,4,3,2,1,0:T(8,128)S(1)}, f32[3,3,1,4,48,128]{5,4,3,2,1,0:T(8,128)S(1)}, u32[]{:S(2)}, u32[]{:S(2)}) collective-permute-start(f32[3,3,1,4,48,128]{5,4,3,2,1,0:T(8,128)S(1)} %pad_maximum_fusion.2), channel_id=1, source_target_pairs={{1,0},{2,1},{3,2},{0,3},{5,4},{6,5},{7,6},{4,7},{9,8},{10,9},{11,1... | collective-permute-start | bytes 2654216 | tf_op jit(solution)/shard_map/ppermute | solution.py:20
  289.0 22.5 %collective-permute-start.17 = (f32[3,3,1,4,48,128]{5,4,3,2,1,0:T(8,128)S(1)}, f32[3,3,1,4,48,128]{5,4,3,2,1,0:T(8,128)S(1)}, u32[]{:S(2)}, u32[]{:S(2)}) collective-permute-start(f32[3,3,1,4,48,128]{5,4,3,2,1,0:T(8,128)S(1)} %pad_maximum_fusion.2), channel_id=1, source_target_pairs={{0,1},{1,2},{2,3},{3,0},{4,5},{5,6},{6,7},{7,4},{8,9},{9,10},{10,1... | collective-permute-start | bytes 2654216 | tf_op jit(solution)/shard_map/ppermute | solution.py:19
  314.9 41.2 %collective-permute-start.19 = (f32[1,1,1,4,48,128]{5,4,3,2,1,0:T(8,128)S(1)}, f32[1,1,1,4,48,128]{5,4,3,2,1,0:T(8,128)S(1)}, u32[]{:S(2)}, u32[]{:S(2)}) collective-permute-start(f32[1,1,1,4,48,128]{5,4,3,2,1,0:T(8,128)S(1)} %get-tuple-element.30), channel_id=1, source_target_pairs={{0,8},{8,16},{16,24},{24,0},{1,9},{9,17},{17,25},{25,1},{2,10},{10... | collective-permute-start | bytes 294920 | tf_op jit(solution)/shard_map/ppermute | solution.py:19
  316.2 39.9 %collective-permute-start.18 = (f32[1,1,1,4,48,128]{5,4,3,2,1,0:T(8,128)S(1)}, f32[1,1,1,4,48,128]{5,4,3,2,1,0:T(8,128)S(1)}, u32[]{:S(2)}, u32[]{:S(2)}) collective-permute-start(f32[1,1,1,4,48,128]{5,4,3,2,1,0:T(8,128)S(1)} %get-tuple-element.30), channel_id=1, source_target_pairs={{8,0},{16,8},{24,16},{0,24},{9,1},{17,9},{25,17},{1,25},{10,2},{18... | collective-permute-start | bytes 294920 | tf_op jit(solution)/shard_map/ppermute | solution.py:20
  356.2 10.2 %collective-permute-start.21 = (f32[3,1,1,4,48,128]{5,4,3,2,1,0:T(8,128)S(1)}, f32[3,1,1,4,48,128]{5,4,3,2,1,0:T(8,128)S(1)}, u32[]{:S(2)}, u32[]{:S(2)}) collective-permute-start(f32[3,1,1,4,48,128]{5,4,3,2,1,0:T(8,128)S(1)} %pad_maximum_fusion.8), channel_id=1, source_target_pairs={{0,4},{4,0},{1,5},{5,1},{2,6},{6,2},{3,7},{7,3},{8,12},{12,8},{9,1... | collective-permute-start | bytes 884744 | tf_op jit(solution)/shard_map/ppermute | solution.py:19
  358.5 12.0 %collective-permute-start.20 = (f32[3,1,1,4,48,128]{5,4,3,2,1,0:T(8,128)S(1)}, f32[3,1,1,4,48,128]{5,4,3,2,1,0:T(8,128)S(1)}, u32[]{:S(2)}, u32[]{:S(2)}) collective-permute-start(f32[3,1,1,4,48,128]{5,4,3,2,1,0:T(8,128)S(1)} %pad_maximum_fusion.8), channel_id=1, source_target_pairs={{4,0},{0,4},{5,1},{1,5},{6,2},{2,6},{7,3},{3,7},{12,8},{8,12},{13,... | collective-permute-start | bytes 884744 | tf_op jit(solution)/shard_map/ppermute | solution.py:20
  370.6 19.5 %collective-permute-start.22 = (f32[3,3,1,4,48,128]{5,4,3,2,1,0:T(8,128)S(1)}, f32[3,3,1,4,48,128]{5,4,3,2,1,0:T(8,128)S(1)}, u32[]{:S(2)}, u32[]{:S(2)}) collective-permute-start(f32[3,3,1,4,48,128]{5,4,3,2,1,0:T(8,128)S(1)} %pad_maximum_fusion.3), channel_id=1, source_target_pairs={{1,0},{2,1},{3,2},{0,3},{5,4},{6,5},{7,6},{4,7},{9,8},{10,9},{11,1... | collective-permute-start | bytes 2654216 | tf_op jit(solution)/shard_map/ppermute | solution.py:20
  370.7 21.5 %collective-permute-start.23 = (f32[3,3,1,4,48,128]{5,4,3,2,1,0:T(8,128)S(1)}, f32[3,3,1,4,48,128]{5,4,3,2,1,0:T(8,128)S(1)}, u32[]{:S(2)}, u32[]{:S(2)}) collective-permute-start(f32[3,3,1,4,48,128]{5,4,3,2,1,0:T(8,128)S(1)} %pad_maximum_fusion.3), channel_id=1, source_target_pairs={{0,1},{1,2},{2,3},{3,0},{4,5},{5,6},{6,7},{7,4},{8,9},{9,10},{10,1... | collective-permute-start | bytes 2654216 | tf_op jit(solution)/shard_map/ppermute | solution.py:19
  395.6 7.3 %collective-permute-start.25 = (f32[1,1,1,4,48,128]{5,4,3,2,1,0:T(8,128)S(1)}, f32[1,1,1,4,48,128]{5,4,3,2,1,0:T(8,128)S(1)}, u32[]{:S(2)}, u32[]{:S(2)}) collective-permute-start(f32[1,1,1,4,48,128]{5,4,3,2,1,0:T(8,128)S(1)} %get-tuple-element.27), channel_id=1, source_target_pairs={{0,8},{8,16},{16,24},{24,0},{1,9},{9,17},{17,25},{25,1},{2,10},{10... | collective-permute-start | bytes 294920 | tf_op jit(solution)/shard_map/ppermute | solution.py:19
  398.3 5.8 %collective-permute-start.24 = (f32[1,1,1,4,48,128]{5,4,3,2,1,0:T(8,128)S(1)}, f32[1,1,1,4,48,128]{5,4,3,2,1,0:T(8,128)S(1)}, u32[]{:S(2)}, u32[]{:S(2)}) collective-permute-start(f32[1,1,1,4,48,128]{5,4,3,2,1,0:T(8,128)S(1)} %get-tuple-element.27), channel_id=1, source_target_pairs={{8,0},{16,8},{24,16},{0,24},{9,1},{17,9},{25,17},{1,25},{10,2},{18... | collective-permute-start | bytes 294920 | tf_op jit(solution)/shard_map/ppermute | solution.py:20
  404.0 48.7 %collective-permute-start.27 = (f32[3,1,1,4,48,128]{5,4,3,2,1,0:T(8,128)S(1)}, f32[3,1,1,4,48,128]{5,4,3,2,1,0:T(8,128)S(1)}, u32[]{:S(2)}, u32[]{:S(2)}) collective-permute-start(f32[3,1,1,4,48,128]{5,4,3,2,1,0:T(8,128)S(1)} %pad_maximum_fusion.9), channel_id=1, source_target_pairs={{0,4},{4,0},{1,5},{5,1},{2,6},{6,2},{3,7},{7,3},{8,12},{12,8},{9,1... | collective-permute-start | bytes 884744 | tf_op jit(solution)/shard_map/ppermute | solution.py:19
  406.1 46.6 %collective-permute-start.26 = (f32[3,1,1,4,48,128]{5,4,3,2,1,0:T(8,128)S(1)}, f32[3,1,1,4,48,128]{5,4,3,2,1,0:T(8,128)S(1)}, u32[]{:S(2)}, u32[]{:S(2)}) collective-permute-start(f32[3,1,1,4,48,128]{5,4,3,2,1,0:T(8,128)S(1)} %pad_maximum_fusion.9), channel_id=1, source_target_pairs={{4,0},{0,4},{5,1},{1,5},{6,2},{2,6},{7,3},{3,7},{12,8},{8,12},{13,... | collective-permute-start | bytes 884744 | tf_op jit(solution)/shard_map/ppermute | solution.py:20
  452.8 18.1 %collective-permute-start.28 = (f32[3,3,1,4,48,128]{5,4,3,2,1,0:T(8,128)S(1)}, f32[3,3,1,4,48,128]{5,4,3,2,1,0:T(8,128)S(1)}, u32[]{:S(2)}, u32[]{:S(2)}) collective-permute-start(f32[3,3,1,4,48,128]{5,4,3,2,1,0:T(8,128)S(1)} %pad_maximum_fusion.4), channel_id=1, source_target_pairs={{1,0},{2,1},{3,2},{0,3},{5,4},{6,5},{7,6},{4,7},{9,8},{10,9},{11,1... | collective-permute-start | bytes 2654216 | tf_op jit(solution)/shard_map/ppermute | solution.py:20
  452.9 22.7 %collective-permute-start.29 = (f32[3,3,1,4,48,128]{5,4,3,2,1,0:T(8,128)S(1)}, f32[3,3,1,4,48,128]{5,4,3,2,1,0:T(8,128)S(1)}, u32[]{:S(2)}, u32[]{:S(2)}) collective-permute-start(f32[3,3,1,4,48,128]{5,4,3,2,1,0:T(8,128)S(1)} %pad_maximum_fusion.4), channel_id=1, source_target_pairs={{0,1},{1,2},{2,3},{3,0},{4,5},{5,6},{6,7},{7,4},{8,9},{9,10},{10,1... | collective-permute-start | bytes 2654216 | tf_op jit(solution)/shard_map/ppermute | solution.py:19
  (2 other events, 1.8 us)
Sparse Core Ops, SparseCore 0:
  14.2 122.0 all-reduce.5
where the time goes:
time: 526 us
  waiting for transfers between devices  287 us (55%)
  blocking collectives  166 us (32%)
  starting transfers between devices  31.9 us (6%)
  matrix products  16.3 us (3%)
  between operations  14.7 us (3%)
  other arithmetic  7.22 us (1%)
    psum x4, blocking collectives, sweep_step(): lax.psum((first[:half] + first[half:], second[:half] - second[half:], pow...  166 us
    psum x1, waiting for transfers between devices, local(): cross = lax.psum(local_cross, ('ta', 'gz', 'xy'))  126 us
    ppermute x15, waiting for transfers between devices, with_halo(): after = lax.ppermute(initial, axis, down)  110 us
    ppermute x15, waiting for transfers between devices, with_halo(): before = lax.ppermute(last, axis, up)  51.3 us
    ppermute x15, starting transfers between devices, with_halo(): before = lax.ppermute(last, axis, up)  20.6 us
    ppermute x15, starting transfers between devices, with_halo(): after = lax.ppermute(initial, axis, down)  11.2 us
  transfers between devices with their start and end apart: 31, of which 25 were waited for; matrix products, arithmetic and copies ran while one was open for 1% of the time, Pallas kernels for 0%

commit v1 on v0

v1 whole, which is shorter than its diff:
```python
import functools

import jax
import jax.numpy as jnp
from jax import lax
from jax.experimental import pallas as pl
from jax.experimental.pallas import tpu as pltpu
from jax.sharding import PartitionSpec as P

SWEEPS = 4
HIGH = lax.Precision.HIGHEST
MESH = pl.DeviceIdType.MESH
F32, BF16 = jnp.float32, jnp.bfloat16


def split(x):
    first = x.astype(BF16)
    x = x - first.astype(F32)
    second = x.astype(BF16)
    return first, second, (x - second.astype(F32)).astype(BF16)


def kernel(
    sizes, dims, links_hbm, v_ref, er_ref, ei_ref, rhs_ref, sol_ref, res_ref,
    links, tail, flat, mats, srcs, acc, fields, halos, w_ref, cfull, cpart, rs_buf, ct_buf,
    ag_buf, at_buf, ap_buf, vw,
    link_sem, halo_send, halo_recv, rs_send, rs_recv, ct_send, ct_recv, ag_send, ag_recv,
    at_send, at_recv, ap_send, ap_recv,
):
    nt, nz, nx = sizes
    ny, dof, lanes = dims
    half = lanes // 2
    plane = nz * nx
    it, iz, ix = lax.axis_index("ta"), lax.axis_index("gz"), lax.axis_index("xy")
    me = iz * nx + ix

    link_copy = pltpu.make_async_copy(links_hbm, links, link_sem)
    link_copy.start()

    def plane_peer(k):
        p = lax.rem(me + k, plane)
        return p, {"ta": it, "gz": lax.div(p, nx), "xy": lax.rem(p, nx)}

    def time_peer(k):
        p = lax.rem(it + k, nt)
        return p, {"ta": p, "gz": iz, "xy": ix}

    barrier = pltpu.get_barrier_semaphore()
    for k in range(1, plane):
        pl.semaphore_signal(barrier, inc=1, device_id=plane_peer(k)[1], device_id_type=MESH)
    for k in range(1, nt):
        pl.semaphore_signal(barrier, inc=1, device_id=time_peer(k)[1], device_id_type=MESH)

    def neighbours(axis, index, n):
        base = {"ta": it, "gz": iz, "xy": ix}
        up, down = dict(base), dict(base)
        up[axis] = lax.rem(index + 1, n)
        down[axis] = lax.rem(index + n - 1, n)
        return up, down

    outgoing, groups, slot = [], {}, 0
    for axis, index, n, d in (("ta", it, nt, 1), ("xy", ix, nx, 3), ("gz", iz, nz, 2)):
        up, down = neighbours(axis, index, n)
        if n == 2:
            outgoing.append((slot, up))
            groups[axis] = [(slot, (d, d + 4))]
            slot += 1
        else:
            outgoing.append((slot, down))
            outgoing.append((slot + 1, up))
            groups[axis] = [(slot, (d,)), (slot + 1, (d + 4,))]
            slot += 2
    far, near = groups["ta"], groups["xy"] + groups["gz"]

    def send_field(rnd, src):
        out = []
        for s, target in outgoing:
            c = pltpu.make_async_remote_copy(
                src_ref=src, dst_ref=halos.at[rnd, s],
                send_sem=halo_send.at[rnd, s], recv_sem=halo_recv.at[rnd, s],
                device_id=target, device_id_type=MESH,
            )
            c.start()
            out.append((s, c))
        return dict(out)

    def share(buf, mine, n, peer, send, recv):
        out = []
        for k in range(1, n):
            c = pltpu.make_async_remote_copy(
                src_ref=buf.at[mine], dst_ref=buf.at[mine],
                send_sem=send.at[k], recv_sem=recv.at[k],
                device_id=peer(k)[1], device_id_type=MESH,
            )
            c.start()
            out.append(c)
        return out

    def recv_all(copies):
        for c in copies:
            c.wait_recv()

    lane = lax.broadcasted_iota(jnp.int32, (1, lanes), 1)
    low = lane < half
    jsign = jnp.where(low, -1.0, 1.0).astype(F32)

    def swap(x):
        return pltpu.roll(x, half, 1)

    pl.semaphore_wait(barrier, plane - 1 + nt - 1)

    sends = []
    v_copies = send_field(0, v_ref)
    sends += list(v_copies.values())

    rows = v_ref[...].reshape(ny * dof, lanes)
    cross = lax.dot_general(
        rows, rhs_ref[...].reshape(ny * dof, lanes), (((0,), (0,)), ((), ())),
        precision=HIGH, preferred_element_type=F32,
    )
    cfull[...] = cross[:half] - jsign * swap(cross[half:])
    part = half // plane
    for p in range(plane):
        cpart[p] = cfull[p * part : (p + 1) * part]
    rs_copies = []
    for k in range(1, plane):
        p, target = plane_peer(k)
        c = pltpu.make_async_remote_copy(
            src_ref=cpart.at[p], dst_ref=rs_buf.at[me],
            send_sem=rs_send.at[k], recv_sem=rs_recv.at[k],
            device_id=target, device_id_type=MESH,
        )
        c.start()
        rs_copies.append(c)
    rs_buf[me] = cpart[me]
    sends += rs_copies

    link_copy.wait()
    tail[...] = jnp.zeros_like(tail)
    for y in range(ny):
        tail[pl.ds(y, 1), :] = links[y, 8:9, :]
    two = 2 * dof
    valid = lane < two

    def pick(ref_load, b, j):
        at = j * two
        base, off = (at // 128) * 128, at % 128
        start = pl.multiple_of(b * (4 * two), 128) + base
        width = 128 if off + two <= 128 else 256
        x = ref_load(pl.ds(start, width))
        if off:
            x = pltpu.roll(x, width - off, 1)
        return jnp.where(valid, x[:, :128], 0.0)

    def relayout(b, carry):
        for g in range(ny + 1):
            load = (lambda w, g=g: links[g, 0:8, w]) if g < ny else (lambda w: tail[:, w])
            for j in range(4):
                flat[pl.ds(g * 8 * dof + 4 * b + j, 8, stride=dof), :] = pick(load, b, j)
        return carry

    lax.fori_loop(0, dof // 4, relayout, 0)

    def direction(y, d):
        r = (y * 8 + d) * dof if d < 8 else (ny * 8 + y) * dof
        return flat[pl.ds(r, dof), :]

    order = [(0,), (4,), (8,)] + [ds for _, ds in near] + [ds for _, ds in far]
    for y in range(ny):
        for m, ds in enumerate(order):
            x = direction(y, ds[0])
            for d in ds[1:]:
                x = x + direction(y, d)
            if ds[0]:
                x = -x
            for i, piece in enumerate(split(x)):
                mats[y, i * dof : (i + 1) * dof, m * 128 : (m + 1) * 128] = piece
    srcs[:, :, two:, :] = jnp.zeros((srcs.shape[0], ny, srcs.shape[2] - two, 3 * lanes), BF16)

    def prepare(m, y, x):
        for i, piece in enumerate(split(x)):
            srcs[m, y, :dof, i * lanes : (i + 1) * lanes] = piece
        for i, piece in enumerate(split(swap(x) * jsign)):
            srcs[m, y, dof:two, i * lanes : (i + 1) * lanes] = piece

    def product(y, m0, blocks):
        right = jnp.concatenate([srcs[s, z] for s, z in blocks], 0)
        left = mats[y, :, m0 * 128 : (m0 + len(blocks)) * 128]
        main = jnp.dot(left, right[:, : 2 * lanes], preferred_element_type=F32)
        small = jnp.dot(left[:dof], right[:, 2 * lanes :], preferred_element_type=F32)
        second = main[dof : 2 * dof]
        small = small + main[2 * dof :, :lanes] + second[:, lanes:]
        return main[:dof, :lanes] + (main[:dof, lanes:] + second[:, :lanes] + small)

    def begin(field):
        for y in range(ny):
            prepare(0, y, field[y])
        for y in range(ny):
            acc[y] = product(y, 0, [(0, y), (0, (y + 1) % ny), (0, (y - 1) % ny)])

    def middle(rnd, copies):
        for i, (s, _) in enumerate(near):
            copies[s].wait_recv()
            for y in range(ny):
                prepare(1 + i, y, halos[rnd, s, y])
        for y in range(ny):
            acc[y] += product(y, 3, [(1 + i, y) for i in range(len(near))])

    def finish(rnd, copies, emit):
        first = 1 + len(near)
        for i, (s, _) in enumerate(far):
            copies[s].wait_recv()
            for y in range(ny):
                prepare(first + i, y, halos[rnd, s, y])
        for y in range(ny):
            t = acc[y] + product(y, 3 + len(near), [(first + i, y) for i in range(len(far))])
            emit(y, t)

    recv_all(rs_copies)
    total = rs_buf[0]
    for p in range(1, plane):
        total = total + rs_buf[p]
    ct_buf[it] = total
    ct_copies = share(ct_buf, it, nt, time_peer, ct_send, ct_recv)
    sends += ct_copies

    begin(v_ref)

    recv_all(ct_copies)
    total = ct_buf[0]
    for p in range(1, nt):
        total = total + ct_buf[p]
    ag_buf[me] = total
    ag_copies = share(ag_buf, me, plane, plane_peer, ag_send, ag_recv)
    sends += ag_copies

    middle(0, v_copies)

    def keep(y, value):
        w_ref[y] = value

    finish(0, v_copies, keep)
    for i, ref in enumerate((v_ref, w_ref)):
        one, other, third = split(ref[...].reshape(ny * dof, lanes))
        for j, piece in enumerate((one, other, one, third)):
            vw[i * ny * dof : (i + 1) * ny * dof, j * lanes : (j + 1) * lanes] = piece

    recv_all(ag_copies)
    for p in range(plane):
        cfull[p * part : (p + 1) * part] = ag_buf[p]
    corr = cfull[...]
    eye = lax.broadcasted_iota(jnp.int32, (half, half), 0) == lax.broadcasted_iota(
        jnp.int32, (half, half), 1
    )
    er = jnp.sum(jnp.where(eye, er_ref[...], 0.0), axis=1, keepdims=True)
    ei = jnp.sum(jnp.where(eye, ei_ref[...], 0.0), axis=1, keepdims=True)
    coef = (corr * er - jsign * swap(corr) * ei) / (er * er + ei * ei)
    b1, b2, b3 = split(jnp.concatenate([coef, jsign * swap(coef)], 0))
    block = jnp.concatenate([b1, b2], 1)
    block = jnp.concatenate([block, block], 0)
    both = jnp.dot(vw[:, : 2 * lanes], block, preferred_element_type=F32)
    small = jnp.dot(
        vw[:, 2 * lanes :], jnp.concatenate([b3, b1], 0), preferred_element_type=F32
    )
    both = both[:, :lanes] + (both[:, lanes:] + small)
    n = ny * dof
    r0 = rhs_ref[...] - both[n:].reshape(ny, dof, lanes)
    fields[0] = r0
    copies = send_field(1, fields.at[0])
    sends += list(copies.values())
    sol_ref[...] = both[:n].reshape(ny, dof, lanes)
    res_ref[...] = r0

    begin(fields.at[0])
    middle(1, copies)

    def to_first(y, value):
        fields[1, y] = value

    finish(1, copies, to_first)

    for sweep in range(SWEEPS):
        image = fields.at[sweep + 1]
        last = sweep + 1 == SWEEPS
        s1 = jnp.zeros((1, lanes), F32)
        s2, s3 = s1, s1
        for y in range(ny):
            f, r = image[y], res_ref[y]
            s1 = s1 + jnp.sum(f * r, axis=0, keepdims=True)
            s2 = s2 + jnp.sum(f * swap(r), axis=0, keepdims=True)
            s3 = s3 + jnp.sum(f * f, axis=0, keepdims=True)
        num = jnp.where(low, s1 + swap(s1), swap(s2) - s2)
        den = s3 + swap(s3)
        row = lax.broadcasted_iota(jnp.int32, (8, lanes), 0)
        tbuf, pbuf = at_buf.at[sweep], ap_buf.at[sweep]
        tbuf[it] = jnp.where(row == 0, num, den)
        t_copies = share(tbuf, it, nt, time_peer, at_send.at[sweep], at_recv.at[sweep])
        sends += t_copies
        if not last:
            copies = send_field(sweep + 2, image)
            sends += list(copies.values())
            begin(image)
        recv_all(t_copies)
        total = tbuf[0]
        for p in range(1, nt):
            total = total + tbuf[p]
        pbuf[me] = total
        p_copies = share(pbuf, me, plane, plane_peer, ap_send.at[sweep], ap_recv.at[sweep])
        sends += p_copies
        if not last:
            middle(sweep + 2, copies)
        recv_all(p_copies)
        total = pbuf[0]
        for p in range(1, plane):
            total = total + pbuf[p]
        a = total[0:1] / total[1:2]
        sa = swap(a)
        ar = jnp.where(low, a, sa)
        ai = jnp.where(low, sa, a) * jsign
        for y in range(ny):
            f, r = image[y], res_ref[y]
            sol_ref[y] = sol_ref[y] + (ar * r + ai * swap(r))
            res_ref[y] = r - (ar * f + ai * swap(f))
        if not last:

            def update(y, value):
                fields[sweep + 2, y] = image[y] - (ar * value + ai * swap(value))

            finish(sweep + 2, copies, update)
    for c in sends:
        c.wait_send()


def local(sizes, links, eigvecs, eig_real, eig_imag, rhs):
    nt, nz, nx = sizes
    plane = nz * nx
    ny, dof, lanes = rhs.shape[3:]
    half = lanes // 2
    field = (ny, dof, lanes)
    ndir = links.shape[4]
    slots = sum(1 if n == 2 else 2 for n in sizes)
    part = half // plane
    rounds = SWEEPS + 1
    vmem, dma = pltpu.VMEM, pltpu.SemaphoreType.DMA
    spec = pl.BlockSpec(memory_space=pltpu.VMEM)
    sol, res = pl.pallas_call(
        functools.partial(kernel, sizes, field),
        out_shape=[jax.ShapeDtypeStruct(field, F32)] * 2,
        in_specs=[pl.BlockSpec(memory_space=pl.ANY)] + [spec] * 4,
        out_specs=[spec] * 2,
        scratch_shapes=[
            vmem((ny, ndir, links.shape[5]), F32),
            vmem((8, links.shape[5]), F32),
            vmem(((ny * 8 + 8) * dof, 128), F32),
            vmem((ny, 3 * dof, (3 + slots) * 128), BF16),
            vmem((1 + slots, ny, 128, 3 * lanes), BF16),
            vmem(field, F32),
            vmem((rounds,) + field, F32),
            vmem((rounds, slots) + field, F32),
            vmem(field, F32),
            vmem((half, lanes), F32),
            vmem((plane, part, lanes), F32),
            vmem((plane, part, lanes), F32),
            vmem((nt, part, lanes), F32),
            vmem((plane, part, lanes), F32),
            vmem((SWEEPS, nt, 8, lanes), F32),
            vmem((SWEEPS, plane, 8, lanes), F32),
            vmem((2 * ny * dof, 4 * lanes), BF16),
            dma,
            dma((rounds, slots)),
            dma((rounds, slots)),
            dma((plane,)),
            dma((plane,)),
            dma((nt,)),
            dma((nt,)),
            dma((plane,)),
            dma((plane,)),
            dma((SWEEPS, nt)),
            dma((SWEEPS, nt)),
            dma((SWEEPS, plane)),
            dma((SWEEPS, plane)),
        ],
        compiler_params=pltpu.CompilerParams(collective_id=0, has_side_effects=True),
    )(
        links.reshape(links.shape[3:]),
        eigvecs.reshape(field),
        eig_real.reshape(1, -1),
        eig_imag.reshape(1, -1),
        rhs.reshape(field),
    )
    return (sol.reshape(rhs.shape), res.reshape(rhs.shape))


def solution(mesh):
    whole = P("ta", "gz", "xy", None, None, None)
    sizes = tuple(mesh.shape[a] for a in ("ta", "gz", "xy"))
    return jax.shard_map(
        functools.partial(local, sizes),
        mesh=mesh,
        in_specs=(whole, whole, P(), P(), whole),
        out_specs=(whole, whole),
        check_vma=False,
    )
```

time: 526 us -> 64.4 us (0.12)
  waiting for transfers between devices: 287 us -> 0 us
  blocking collectives: 166 us -> 0 us
  Pallas kernels: 0 us -> 58.1 us
  starting transfers between devices: 31.9 us -> 0 us
  matrix products: 16.3 us -> 0 us
  between operations: 14.7 us -> 0.64 us
  other arithmetic: 7.22 us -> 0 us
    psum x4 -> x0, blocking collectives: 166 us -> none  [sweep_step(): lax.psum((first[:half] + first[half:], second[:half] - second[half:], pow...]
    ppermute x30 -> x0, waiting for transfers between devices: 161 us -> none  [the longest x15 110 us: with_halo(): after = lax.ppermute(initial, axis, down)]
    psum x1 -> x0, waiting for transfers between devices: 126 us -> none  [local(): cross = lax.psum(local_cross, ('ta', 'gz', 'xy'))]
    pallas_call x0 -> x1, Pallas kernels: none -> 58.1 us  [local(): pl.pallas_call(functools.partial(kernel, sizes, field), out_shape=[jax.Sh...]
    ppermute x30 -> x0, starting transfers between devices: 31.8 us -> none  [the longest x15 20.6 us: with_halo(): before = lax.ppermute(last, axis, up)]
    dot_general x12 -> x0, matrix products: 16.3 us -> none  [the longest x5 7.59 us: operate(): jnp.einsum('tzxydoi,tzxydic->tzxyoc', links[..., dof:], stacked, precisio...]
  transfers between devices with their start and end apart: 31 -> 0, of which waited for: 25 -> 0; matrix products, arithmetic and copies ran while one was open for 1% -> 0% of each run, Pallas kernels for 0% -> 0%
where the time goes in v1:
time: 64.4 us; the launch traced here: 64.1 us
  Pallas kernels  58.1 us (90%)
  local copies, waits for them, and re-layouts  5.43 us (8%)
    pallas_call x1, Pallas kernels, local(): pl.pallas_call(functools.partial(kernel, sizes, field), out_shape=[jax.Sh...  58.1 us
    unnamed x3, local copies, waits for them, and re-layouts  5.43 us

profile of v1, /device:TPU:0, one launch (start us, length us, event | category | flops | bytes accessed | tf_op | source)
XLA Modules:
  0.0 64.1 jit_solution(12196053645571465074)
XLA Ops:
  0.6 2.3 %copy.9 = f32[1,1,1,4,9,4608]{5,4,3,2,1,0:T(8,128)} copy(f32[1,1,1,4,9,4608]{5,3,4,2,1,0:T(4,128)} %param.5) | data formatting | bytes 1327104 | tf_op args[0]
  3.0 58.1 %shard_map.68 = (f32[4,48,128]{2,1,0:T(8,128)}, f32[4,48,128]{2,1,0:T(8,128)}) custom-call(f32[4,9,4608]{2,1,0:T(8,128)} %bitcast.9, f32[4,48,128]{2,1,0:T(8,128)} %bitcast.10, f32[1,64]{1,0:T(1,128)} %bitcast.14, f32[1,64]{1,0:T(1,128)} %bitcast.15, f32[4,48,128]{2,1,0:T(8,128)} %bitcast.11), custom_call_target="tpu_custom_call" | custom-call | tf_op jit(solution)/shard_map/pallas_call | solution.py:346
  61.1 1.5 %copy.12 = f32[1,1,1,4,48,128]{5,4,3,2,1,0:T(8,128)} copy(f32[1,1,1,4,48,128]{5,4,3,2,1,0:T(8,128)} %bitcast.13) | data formatting | bytes 196608
  62.6 1.5 %copy.13 = f32[1,1,1,4,48,128]{5,4,3,2,1,0:T(8,128)} copy(f32[1,1,1,4,48,128]{5,4,3,2,1,0:T(8,128)} %bitcast.12) | data formatting | bytes 196608

commit v2 on v1

--- a/solution.py
+++ b/solution.py
@@ -8,6 +8,7 @@
 from jax.sharding import PartitionSpec as P
 
 SWEEPS = 4
+DIRECT = 32
 HIGH = lax.Precision.HIGHEST
 MESH = pl.DeviceIdType.MESH
 F32, BF16 = jnp.float32, jnp.bfloat16
@@ -22,7 +23,7 @@
 
 def kernel(
     sizes, dims, links_hbm, v_ref, er_ref, ei_ref, rhs_ref, sol_ref, res_ref,
-    links, tail, flat, mats, srcs, acc, fields, halos, w_ref, cfull, cpart, rs_buf, ct_buf,
+    links, flat, mats, srcs, acc, fields, halos, w_ref, cfull, cpart, rs_buf, ct_buf,
     ag_buf, at_buf, ap_buf, vw,
     link_sem, halo_send, halo_recv, rs_send, rs_recv, ct_send, ct_recv, ag_send, ag_recv,
     at_send, at_recv, ap_send, ap_recv,
@@ -45,11 +46,23 @@
         p = lax.rem(it + k, nt)
         return p, {"ta": p, "gz": iz, "xy": ix}
 
+    everyone = nt * plane
+    rank = it * plane + me
+
+    def any_peer(k):
+        p = lax.rem(rank + k, everyone)
+        r = lax.rem(p, plane)
+        return p, {"ta": lax.div(p, plane), "gz": lax.div(r, nx), "xy": lax.rem(r, nx)}
+
+    direct = everyone <= DIRECT
+    if direct:
+        greeted = [any_peer(k)[1] for k in range(1, everyone)]
+    else:
+        greeted = [plane_peer(k)[1] for k in range(1, plane)]
+        greeted += [time_peer(k)[1] for k in range(1, nt)]
     barrier = pltpu.get_barrier_semaphore()
-    for k in range(1, plane):
-        pl.semaphore_signal(barrier, inc=1, device_id=plane_peer(k)[1], device_id_type=MESH)
-    for k in range(1, nt):
-        pl.semaphore_signal(barrier, inc=1, device_id=time_peer(k)[1], device_id_type=MESH)
+    for target in greeted:
+        pl.semaphore_signal(barrier, inc=1, device_id=target, device_id_type=MESH)
 
     def neighbours(axis, index, n):
         base = {"ta": it, "gz": iz, "xy": ix}
@@ -62,27 +75,39 @@
     for axis, index, n, d in (("ta", it, nt, 1), ("xy", ix, nx, 3), ("gz", iz, nz, 2)):
         up, down = neighbours(axis, index, n)
         if n == 2:
-            outgoing.append((slot, up))
+            outgoing.append((axis, slot, up))
             groups[axis] = [(slot, (d, d + 4))]
             slot += 1
         else:
-            outgoing.append((slot, down))
-            outgoing.append((slot + 1, up))
+            turn = jnp.where(index == n - 1, 1, 0)
+            for t in (turn, 1 - turn):
+                target = dict(up)
+                target[axis] = lax.rem(index + n - 1 + 2 * t, n)
+                outgoing.append((axis, slot + t, target))
             groups[axis] = [(slot, (d,)), (slot + 1, (d + 4,))]
             slot += 2
     far, near = groups["ta"], groups["xy"] + groups["gz"]
 
-    def send_field(rnd, src):
+    def send_field(rnd, src, axes=("ta", "xy", "gz")):
         out = []
-        for s, target in outgoing:
+        for axis, s, target in outgoing:
+            if axis not in axes:
+                continue
             c = pltpu.make_async_remote_copy(
                 src_ref=src, dst_ref=halos.at[rnd, s],
                 send_sem=halo_send.at[rnd, s], recv_sem=halo_recv.at[rnd, s],
                 device_id=target, device_id_type=MESH,
             )
             c.start()
-            out.append((s, c))
-        return dict(out)
+            out.append(c)
+        return out
+
+    def arrived(rnd, s):
+        pltpu.make_async_remote_copy(
+            src_ref=v_ref, dst_ref=halos.at[rnd, s],
+            send_sem=halo_send.at[rnd, s], recv_sem=halo_recv.at[rnd, s],
+            device_id=outgoing[0][2], device_id_type=MESH,
+        ).wait_recv()
 
     def share(buf, mine, n, peer, send, recv):
         out = []
@@ -100,6 +125,13 @@
         for c in copies:
             c.wait_recv()
 
+    def add_slots(buf, n):
+        parts = [buf[p] for p in range(n)]
+        while len(parts) > 1:
+            odd = parts[len(parts) // 2 * 2 :]
+            parts = [a + b for a, b in zip(parts[::2], parts[1::2])] + odd
+        return parts[0]
+
     lane = lax.broadcasted_iota(jnp.int32, (1, lanes), 1)
     low = lane < half
     jsign = jnp.where(low, -1.0, 1.0).astype(F32)
@@ -107,12 +139,7 @@
     def swap(x):
         return pltpu.roll(x, half, 1)
 
-    pl.semaphore_wait(barrier, plane - 1 + nt - 1)
-
     sends = []
-    v_copies = send_field(0, v_ref)
-    sends += list(v_copies.values())
-
     rows = v_ref[...].reshape(ny * dof, lanes)
     cross = lax.dot_general(
         rows, rhs_ref[...].reshape(ny * dof, lanes), (((0,), (0,)), ((), ())),
@@ -122,6 +149,7 @@
     part = half // plane
     for p in range(plane):
         cpart[p] = cfull[p * part : (p + 1) * part]
+    pl.semaphore_wait(barrier, len(greeted))
     rs_copies = []
     for k in range(1, plane):
         p, target = plane_peer(k)
@@ -134,36 +162,34 @@
         rs_copies.append(c)
     rs_buf[me] = cpart[me]
     sends += rs_copies
+    sends += send_field(0, v_ref, ("xy", "gz"))
 
     link_copy.wait()
-    tail[...] = jnp.zeros_like(tail)
-    for y in range(ny):
-        tail[pl.ds(y, 1), :] = links[y, 8:9, :]
     two = 2 * dof
     valid = lane < two
 
-    def pick(ref_load, b, j):
+    def pick(pair, b, j):
         at = j * two
         base, off = (at // 128) * 128, at % 128
         start = pl.multiple_of(b * (4 * two), 128) + base
         width = 128 if off + two <= 128 else 256
-        x = ref_load(pl.ds(start, width))
+        x = [links[d, :, pl.ds(start, width)] for d in pair]
+        x = jnp.concatenate(x, 0) if len(x) > 1 else x[0]
         if off:
             x = pltpu.roll(x, width - off, 1)
         return jnp.where(valid, x[:, :128], 0.0)
 
     def relayout(b, carry):
-        for g in range(ny + 1):
-            load = (lambda w, g=g: links[g, 0:8, w]) if g < ny else (lambda w: tail[:, w])
+        for pair in ((0, 1), (2, 3), (4, 5), (6, 7), (8,)):
             for j in range(4):
-                flat[pl.ds(g * 8 * dof + 4 * b + j, 8, stride=dof), :] = pick(load, b, j)
+                row = pair[0] * ny * dof + 4 * b + j
+                flat[pl.ds(row, len(pair) * ny, stride=dof), :] = pick(pair, b, j)
         return carry
 
     lax.fori_loop(0, dof // 4, relayout, 0)
 
     def direction(y, d):
-        r = (y * 8 + d) * dof if d < 8 else (ny * 8 + y) * dof
-        return flat[pl.ds(r, dof), :]
+        return flat[pl.ds((d * ny + y) * dof, dof), :]
 
     order = [(0,), (4,), (8,)] + [ds for _, ds in near] + [ds for _, ds in far]
     for y in range(ny):
@@ -198,18 +224,18 @@
         for y in range(ny):
             acc[y] = product(y, 0, [(0, y), (0, (y + 1) % ny), (0, (y - 1) % ny)])
 
-    def middle(rnd, copies):
+    def middle(rnd):
         for i, (s, _) in enumerate(near):
-            copies[s].wait_recv()
+            arrived(rnd, s)
             for y in range(ny):
                 prepare(1 + i, y, halos[rnd, s, y])
         for y in range(ny):
             acc[y] += product(y, 3, [(1 + i, y) for i in range(len(near))])
 
-    def finish(rnd, copies, emit):
+    def finish(rnd, emit):
         first = 1 + len(near)
         for i, (s, _) in enumerate(far):
-            copies[s].wait_recv()
+            arrived(rnd, s)
             for y in range(ny):
                 prepare(first + i, y, halos[rnd, s, y])
         for y in range(ny):
@@ -223,6 +249,7 @@
     ct_buf[it] = total
     ct_copies = share(ct_buf, it, nt, time_peer, ct_send, ct_recv)
     sends += ct_copies
+    sends += send_field(0, v_ref, ("ta",))
 
     begin(v_ref)
 
@@ -234,12 +261,12 @@
     ag_copies = share(ag_buf, me, plane, plane_peer, ag_send, ag_recv)
     sends += ag_copies
 
-    middle(0, v_copies)
+    middle(0)
 
     def keep(y, value):
         w_ref[y] = value
 
-    finish(0, v_copies, keep)
+    finish(0, keep)
     for i, ref in enumerate((v_ref, w_ref)):
         one, other, third = split(ref[...].reshape(ny * dof, lanes))
         for j, piece in enumerate((one, other, one, third)):
@@ -266,18 +293,17 @@
     n = ny * dof
     r0 = rhs_ref[...] - both[n:].reshape(ny, dof, lanes)
     fields[0] = r0
-    copies = send_field(1, fields.at[0])
-    sends += list(copies.values())
+    sends += send_field(1, fields.at[0])
     sol_ref[...] = both[:n].reshape(ny, dof, lanes)
     res_ref[...] = r0
 
     begin(fields.at[0])
-    middle(1, copies)
+    middle(1)
 
     def to_first(y, value):
         fields[1, y] = value
 
-    finish(1, copies, to_first)
+    finish(1, to_first)
 
     for sweep in range(SWEEPS):
         image = fields.at[sweep + 1]
@@ -291,28 +317,27 @@
             s3 = s3 + jnp.sum(f * f, axis=0, keepdims=True)
         num = jnp.where(low, s1 + swap(s1), swap(s2) - s2)
         den = s3 + swap(s3)
-        row = lax.broadcasted_iota(jnp.int32, (8, lanes), 0)
+        row = lax.broadcasted_iota(jnp.int32, (2, lanes), 0)
         tbuf, pbuf = at_buf.at[sweep], ap_buf.at[sweep]
-        tbuf[it] = jnp.where(row == 0, num, den)
-        t_copies = share(tbuf, it, nt, time_peer, at_send.at[sweep], at_recv.at[sweep])
+        mine, n, peer = (rank, everyone, any_peer) if direct else (it, nt, time_peer)
+        tbuf[mine] = jnp.where(row == 0, num, den)
+        t_copies = share(tbuf, mine, n, peer, at_send.at[sweep], at_recv.at[sweep])
         sends += t_copies
         if not last:
-            copies = send_field(sweep + 2, image)
-            sends += list(copies.values())
+            sends += send_field(sweep + 2, image)
             begin(image)
+        if direct and not last:
+            middle(sweep + 2)
         recv_all(t_copies)
-        total = tbuf[0]
-        for p in range(1, nt):
-            total = total + tbuf[p]
-        pbuf[me] = total
-        p_copies = share(pbuf, me, plane, plane_peer, ap_send.at[sweep], ap_recv.at[sweep])
-        sends += p_copies
-        if not last:
-            middle(sweep + 2, copies)
-        recv_all(p_copies)
-        total = pbuf[0]
-        for p in range(1, plane):
-            total = total + pbuf[p]
+        total = add_slots(tbuf, n)
+        if not direct:
+            pbuf[me] = total
+            p_copies = share(pbuf, me, plane, plane_peer, ap_send.at[sweep], ap_recv.at[sweep])
+            sends += p_copies
+            if not last:
+                middle(sweep + 2)
+            recv_all(p_copies)
+            total = add_slots(pbuf, plane)
         a = total[0:1] / total[1:2]
         sa = swap(a)
         ar = jnp.where(low, a, sa)
@@ -326,9 +351,14 @@
             def update(y, value):
                 fields[sweep + 2, y] = image[y] - (ar * value + ai * swap(value))
 
-            finish(sweep + 2, copies, update)
+            finish(sweep + 2, update)
     for c in sends:
         c.wait_send()
+
+
+def hand_over(a_ref, b_ref, sol_ref, res_ref):
+    sol_ref[...] = a_ref[...]
+    res_ref[...] = b_ref[...]
 
 
 def local(sizes, links, eigvecs, eig_real, eig_imag, rhs):
@@ -341,6 +371,7 @@
     slots = sum(1 if n == 2 else 2 for n in sizes)
     part = half // plane
     rounds = SWEEPS + 1
+    first = nt * plane if nt * plane <= DIRECT else nt
     vmem, dma = pltpu.VMEM, pltpu.SemaphoreType.DMA
     spec = pl.BlockSpec(memory_space=pltpu.VMEM)
     sol, res = pl.pallas_call(
@@ -349,9 +380,8 @@
         in_specs=[pl.BlockSpec(memory_space=pl.ANY)] + [spec] * 4,
         out_specs=[spec] * 2,
         scratch_shapes=[
-            vmem((ny, ndir, links.shape[5]), F32),
-            vmem((8, links.shape[5]), F32),
-            vmem(((ny * 8 + 8) * dof, 128), F32),
+            vmem((ndir, ny, links.shape[5]), F32),
+            vmem((ndir * ny * dof, 128), F32),
             vmem((ny, 3 * dof, (3 + slots) * 128), BF16),
             vmem((1 + slots, ny, 128, 3 * lanes), BF16),
             vmem(field, F32),
@@ -363,8 +393,8 @@
             vmem((plane, part, lanes), F32),
             vmem((nt, part, lanes), F32),
             vmem((plane, part, lanes), F32),
-            vmem((SWEEPS, nt, 8, lanes), F32),
-            vmem((SWEEPS, plane, 8, lanes), F32),
+            vmem((SWEEPS, first, 2, lanes), F32),
+            vmem((SWEEPS, plane, 2, lanes), F32),
             vmem((2 * ny * dof, 4 * lanes), BF16),
             dma,
             dma((rounds, slots)),
@@ -375,19 +405,25 @@
             dma((nt,)),
             dma((plane,)),
             dma((plane,)),
-            dma((SWEEPS, nt)),
-            dma((SWEEPS, nt)),
+            dma((SWEEPS, first)),
+            dma((SWEEPS, first)),
             dma((SWEEPS, plane)),
             dma((SWEEPS, plane)),
         ],
         compiler_params=pltpu.CompilerParams(collective_id=0, has_side_effects=True),
     )(
-        links.reshape(links.shape[3:]),
+        links.reshape(links.shape[3:]).transpose(1, 0, 2),
         eigvecs.reshape(field),
         eig_real.reshape(1, -1),
         eig_imag.reshape(1, -1),
         rhs.reshape(field),
     )
+    sol, res = pl.pallas_call(
+        hand_over,
+        out_shape=[jax.ShapeDtypeStruct(field, F32)] * 2,
+        in_specs=[spec] * 2,
+        out_specs=[spec] * 2,
+    )(sol, res)
     return (sol.reshape(rhs.shape), res.reshape(rhs.shape))
 
 

time: 64.4 us -> 57.5 us (0.89)
  local copies, waits for them, and re-layouts: 5.43 us -> 0 us
  Pallas kernels: 58.1 us -> 56.6 us
    unnamed x3 -> x0, local copies, waits for them, and re-layouts: 5.43 us -> none
    pallas_call x1, Pallas kernels: 58.1 us -> 55 us  [local(): pl.pallas_call(functools.partial(kernel, sizes, field), out_shape=[jax.Sh...]
    pallas_call x0 -> x1, Pallas kernels: none -> 1.62 us  [local(): pl.pallas_call(hand_over, out_shape=[jax.ShapeDtypeStruct(field, F32)] *...]
where the time goes in v2:
time: 57.5 us; the launch traced here: 57.3 us
  Pallas kernels  56.6 us (98%)
  between operations  0.64 us (1%)
    pallas_call x1, Pallas kernels, local(): pl.pallas_call(functools.partial(kernel, sizes, field), out_shape=[jax.Sh...  55 us
    pallas_call x1, Pallas kernels, local(): pl.pallas_call(hand_over, out_shape=[jax.ShapeDtypeStruct(field, F32)] *...  1.62 us

profile of v2, /device:TPU:0, one launch (start us, length us, event | category | flops | bytes accessed | tf_op | source)
XLA Modules:
  0.0 57.3 jit_solution(7744305886457963179)
XLA Ops:
  0.6 55.0 %shard_map.68 = (f32[4,48,128]{2,1,0:T(8,128)}, f32[4,48,128]{2,1,0:T(8,128)}) custom-call(f32[9,4,4608]{2,1,0:T(4,128)} %bitcast.9, f32[4,48,128]{2,1,0:T(8,128)} %bitcast.10, f32[1,64]{1,0:T(1,128)} %bitcast.12, f32[1,64]{1,0:T(1,128)} %bitcast.13, f32[4,48,128]{2,1,0:T(8,128)} %bitcast.11), custom_call_target="tpu_custom_call" | custom-call | tf_op jit(solution)/shard_map/pallas_call | solution.py:377
  55.7 1.6 %shard_map.69 = (f32[4,48,128]{2,1,0:T(8,128)}, f32[4,48,128]{2,1,0:T(8,128)}) custom-call(f32[4,48,128]{2,1,0:T(8,128)} %get-tuple-element.6.a_ref, f32[4,48,128]{2,1,0:T(8,128)} %get-tuple-element.7.b_ref), custom_call_target="tpu_custom_call" | custom-call | tf_op jit(solution)/shard_map/pallas_call | solution.py:421
